TPU v7x, 512 devices: a whole 4x8x8 slice. The times are simulated.
512 devices in a mesh: dp: 16 (over z, core), fsdp: 32 (over x, y).
Axes of the slice: x: 4, y: 8, z: 8, core: 2. Of those that a mesh axis runs over, the one named last changes fastest.
Arguments:
- replica_grads: bfloat16 [16, 8192, 4096], P('dp', 'fsdp'), may hold values from -4 to 4
- slot_table: int32 [32], replicated, may hold values from 0 to 63, as said below
- left_gram_state: float32 [64, 4, 16, 16, 1024], P('fsdp', None, 'dp')
- right_gram_state: float32 [64, 4, 16, 16, 1024], P('fsdp', None, 'dp')
- left_inverse_root: bfloat16 [64, 4, 16, 16, 1024], P('fsdp', None, 'dp')
- right_inverse_root: bfloat16 [64, 4, 16, 16, 1024], P('fsdp', None, 'dp')
Outputs:
- direction: bfloat16 [32, 16, 16, 4096], P('fsdp', 'dp')
- left_new: float32 [64, 4, 16, 16, 1024], P('fsdp', None, 'dp')
- right_new: float32 [64, 4, 16, 16, 1024], P('fsdp', None, 'dp')
Inputs may be any that keep to these rules, and one draw needn't show every extreme that they name: `slot_table`: the entries are distinct; slot v belongs to owner v // 2 of the flat shards' devices; some owner holds 2 blocks.
All inputs are finite; a program needn't handle non-finite values.
Results may differ from a plain program's by a relative error of at most 0.02.
Values may be sent and summed in bfloat16 or wider, within the bound.
No kernel may reach another device: no remote copies, remote signals or barrier semaphores. Data moves between devices by JAX's collectives and lax.ppermute only.
A program may use at most 128 MiB of HBM per device.

v0:
```python
import jax
import jax.numpy as jnp
from jax import lax
from jax.sharding import PartitionSpec as P


def on_device(
    replica_grads,
    slot_table,
    left_gram_state,
    right_gram_state,
    left_inverse_root,
    right_inverse_root,
):
    slots_here = left_gram_state.shape[0]
    sub_blocks = left_gram_state.shape[1]
    strip_rows = left_gram_state.shape[3]
    block_size = left_gram_state.shape[4]
    band_rows = replica_grads.shape[1]
    model_width = replica_grads.shape[2]
    per_band = model_width // block_size
    shards = lax.axis_size("fsdp")
    groups = lax.axis_size("dp")
    total_slots = shards * slots_here
    block_count = slot_table.shape[0]
    band_index = lax.axis_index("fsdp")
    strip_index = lax.axis_index("dp")
    slot_indices = jnp.arange(total_slots, dtype=jnp.int32)
    right_entire = lax.all_gather(right_inverse_root, "dp", axis=2, tiled=True).reshape(
        slots_here, block_size, block_size
    )
    summed = lax.psum_scatter(
        replica_grads[0].astype(jnp.float32).astype(jnp.bfloat16),
        "dp",
        scatter_dimension=0,
        tiled=True,
    )
    row_block = band_index * band_rows // block_size
    targets = lax.dynamic_slice_in_dim(slot_table, row_block * per_band, per_band, 0)
    chooser = (targets[:, None] == slot_indices[None, :]).astype(jnp.bfloat16)
    own_slots = band_index * slots_here + jnp.arange(slots_here, dtype=jnp.int32)
    holder = slot_table[None, :] == own_slots[:, None]
    block_of = jnp.sum(
        jnp.where(holder, jnp.arange(block_count, dtype=jnp.int32)[None, :], 0), axis=1
    )
    first_band = block_of // per_band * sub_blocks
    outgoing = jnp.einsum(
        "cn,tcb->ntb",
        chooser,
        summed.reshape(strip_rows, per_band, block_size),
        preferred_element_type=jnp.float32,
    ).astype(jnp.bfloat16)
    outgoing = outgoing.reshape(shards, slots_here, strip_rows, block_size)
    arrived = lax.all_to_all(outgoing, "fsdp", split_axis=0, concat_axis=0, tiled=True)
    owned_rows = jax.vmap(
        lambda portion, offset: lax.dynamic_slice_in_dim(portion, offset, sub_blocks, 0),
        in_axes=(1, 0),
    )(arrived, first_band)
    owned_rows = owned_rows.reshape(slots_here, sub_blocks, 1, strip_rows, block_size)
    entire = lax.all_gather(owned_rows, "dp", axis=2, tiled=True).reshape(
        slots_here, block_size, block_size
    )
    my_rows = owned_rows.reshape(slots_here, sub_blocks * strip_rows, block_size)
    left_gram = jnp.einsum("mrc,mnc->mrn", my_rows, entire, preferred_element_type=jnp.float32)
    left_new = left_gram_state + (left_gram / block_size).reshape(left_gram_state.shape)
    my_columns = lax.dynamic_index_in_dim(
        entire.reshape(slots_here, block_size, sub_blocks, groups, strip_rows),
        strip_index,
        3,
        keepdims=False,
    )
    my_columns = my_columns.reshape(slots_here, block_size, sub_blocks * strip_rows)
    right_gram = jnp.einsum("mnr,mnc->mrc", my_columns, entire, preferred_element_type=jnp.float32)
    right_new = right_gram_state + (right_gram / block_size).reshape(right_gram_state.shape)
    left_rows = left_inverse_root.reshape(slots_here, sub_blocks * strip_rows, block_size)
    mixed_rows = jnp.einsum(
        "mrn,mnc->mrc", left_rows, entire, preferred_element_type=jnp.float32
    ).astype(jnp.bfloat16)
    result = jnp.einsum(
        "mrn,mnc->mrc", mixed_rows, right_entire, preferred_element_type=jnp.float32
    )
    outcome = result.astype(jnp.bfloat16).reshape(slots_here, sub_blocks, strip_rows, block_size)
    homeward = jax.vmap(
        lambda portion, offset: lax.dynamic_update_slice_in_dim(
            jnp.zeros((shards, strip_rows, block_size), jnp.bfloat16), portion, offset, 0
        ),
        out_axes=1,
    )(outcome, first_band)
    returned = lax.all_to_all(homeward, "fsdp", split_axis=0, concat_axis=0, tiled=True)
    picked = jnp.einsum(
        "cn,ntb->tcb",
        chooser,
        returned.reshape(total_slots, strip_rows, block_size),
        preferred_element_type=jnp.float32,
    ).astype(jnp.bfloat16)
    direction = picked.reshape(1, 1, strip_rows, model_width)
    return (direction, left_new, right_new)


def solution(mesh):
    placed = (
        P("dp", "fsdp", None),
        P(),
        P("fsdp", None, "dp", None, None),
        P("fsdp", None, "dp", None, None),
        P("fsdp", None, "dp", None, None),
        P("fsdp", None, "dp", None, None),
    )
    return jax.shard_map(
        on_device,
        mesh=mesh,
        in_specs=placed,
        out_specs=(
            P("fsdp", "dp", None, None),
            P("fsdp", None, "dp", None, None),
            P("fsdp", None, "dp", None, None),
        ),
        check_vma=False,
    )
```

profile of v0, /device:TPU:16, one launch (start us, length us, event | category | flops | bytes accessed | tf_op | source)
XLA Modules:
  0.0 276.2 jit_solution(1561728517146626942)
XLA Ops:
  7.2 0.7 reduce-scatter.2.cloned.1.call-update
  8.0 0.7 all-gather.4.cloned.1.call-update
  8.7 0.7 dynamic_slice.7
  9.4 69.5 %reduce-scatter.2.cloned.1.call-done = bf16[16,4096]{1,0:T(8,128)(2,1)} async-done(((bf16[256,4096]{1,0:T(8,128)(2,1)}), bf16[16,4096]{1,0:T(8,128)(2,1)}) %reduce-scatter.2.cloned.1.call-update) | async-done | bytes 131088 | tf_op jit(solution)/shard_map/reduce_scatter | solution.py:32
  78.9 1.0 reshape.110
  79.9 0.8 convolution_convert_fusion
  80.7 2.5 copy.35
  83.2 9.8 %all-to-all-start = ((bf16[32,2,16,1024]{3,2,1,0:T(8,128)(2,1)}), bf16[32,2,16,1024]{3,2,1,0:T(8,128)(2,1)S(1)}, u32[]{:S(2)}, u32[]{:S(2)}) async-start(bf16[32,2,16,1024]{3,2,1,0:T(8,128)(2,1)} %bitcast.3), calls=%async_computation.1 | async-start | bytes 4194304 | tf_op jit(solution)/shard_map/all_to_all | solution.py:54
  93.3 45.8 %all-to-all-done = bf16[32,2,16,1024]{3,2,1,0:T(8,128)(2,1)S(1)} async-done(((bf16[32,2,16,1024]{3,2,1,0:T(8,128)(2,1)}), bf16[32,2,16,1024]{3,2,1,0:T(8,128)(2,1)S(1)}, u32[]{:S(2)}, u32[]{:S(2)}) %all-to-all-start) | async-done | bytes 2097184 | tf_op jit(solution)/shard_map/all_to_all | solution.py:54
  139.1 1.3 gather_fusion
  140.6 42.7 %all-gather.6.cloned.1.call-done = bf16[2,4,256,1024]{3,2,1,0:T(8,128)(2,1)} async-done(((bf16[2,4,16,1024]{3,2,1,0:T(8,128)(2,1)}), bf16[2,4,256,1024]{3,2,1,0:T(8,128)(2,1)}) %all-gather.6.cloned.1.call-update) | async-done | bytes 4194320 | tf_op jit(solution)/shard_map/all_gather | solution.py:60
  183.4 5.1 %convolution_convert_fusion.2 = bf16[2,64,1024]{2,1,0:T(8,128)(2,1)S(1)} fusion(bf16[2,1024,1024]{2,1,0:T(8,128)(2,1)} %bitcast.80, bf16[2,64,1024]{2,1,0:T(8,128)(2,1)S(1)} %bitcast.75, bf16[2,1024,1024]{2,1,0:T(8,128)(2,1)} %bitcast.76), kind=kOutput, calls=%fused_computation.12 | convolution fusion | flops 537133056 | bytes 8912896 | tf_op jit(solution)/shard_map/mrn,mnc->mrc/dot_general | solution.py:79
  188.4 1.6 broadcast_in_dim.16.clone
  190.0 17.4 %while.1 = (s32[]{:T(128)}, bf16[2,32,16,1024]{3,2,0,1:T(8,128)(2,1)}, s32[2,4]{1,0:T(2,128)S(1)}, bf16[2,4,16,1024]{3,2,1,0:T(8,128)(2,1)S(1)}, s32[]{:T(128)}, /*index=5*/s32[4]{0:T(128)S(1)}) while((s32[]{:T(128)}, bf16[2,32,16,1024]{3,2,0,1:T(8,128)(2,1)}, s32[2,4]{1,0:T(2,128)S(1)}, bf16[2,4,16,1024]{3,2,1,0:T(8,128)(2,1)S(1)}, s32[]{:T(128)}, ...), condition=%wide.while_cond, body=%wide.while_body.sunk | while | flops 65565 | bytes 657586 | solution.py:84
  190.7 3.3 %and_reduce_fusion.2 = pred[]{:T(512)} fusion(s32[4]{0:T(128)S(1)} %get-tuple-element.91, s32[1]{0:T(128)} %bitcast.71, s32[1]{0:T(128)} %bitcast.72, s32[1]{0:T(128)} %bitcast.73, s32[1]{0:T(128)} %bitcast.74), kind=kLoop, calls=%fused_computation.3.clone.1 | loop fusion | flops 27 | bytes 33 | tf_op jit(solution)/shard_map/vmap(vmap())/scatter
  194.0 2.2 constant_dynamic-slice_fusion.6
  196.2 2.6 bitcast_dynamic-update-slice_fusion.2
  198.8 0.7 fusion.24
  199.4 3.3 %and_reduce_fusion.2 = pred[]{:T(512)} fusion(s32[4]{0:T(128)S(1)} %get-tuple-element.91, s32[1]{0:T(128)} %bitcast.71, s32[1]{0:T(128)} %bitcast.72, s32[1]{0:T(128)} %bitcast.73, s32[1]{0:T(128)} %bitcast.74), kind=kLoop, calls=%fused_computation.3.clone.1 | loop fusion | flops 27 | bytes 33 | tf_op jit(solution)/shard_map/vmap(vmap())/scatter
  202.7 2.2 constant_dynamic-slice_fusion.6
  204.9 2.6 bitcast_dynamic-update-slice_fusion.2
  207.5 9.8 %all-to-all-start.1 = ((bf16[32,2,16,1024]{3,2,1,0:T(8,128)(2,1)}), bf16[32,2,16,1024]{3,2,1,0:T(8,128)(2,1)S(1)}, u32[]{:S(2)}, u32[]{:S(2)}) async-start(bf16[32,2,16,1024]{3,2,1,0:T(8,128)(2,1)} %bitcast.10), calls=%async_computation.2 | async-start | bytes 4194304 | tf_op jit(solution)/shard_map/all_to_all | solution.py:89
  217.3 7.5 %copy.33 = bf16[2,4,256,1024]{2,1,3,0:T(4,128)(2,1)} copy(bf16[2,4,256,1024]{3,2,1,0:T(8,128)(2,1)} %all-gather.6.cloned.1.call-done) | data formatting | bytes 8388608 | tf_op jit(solution)/shard_map/all_gather | solution.py:60
  224.8 7.7 %reshape_reshape.7 = bf16[2,1024,4,16,16]{1,4,3,2,0:T(8,128)(2,1)} reshape(bf16[2,4,256,1024]{2,1,3,0:T(4,128)(2,1)} %copy.33) | data formatting | bytes 8388608 | tf_op jit(solution)/shard_map/reshape;reshape | solution.py:67
  232.6 1.1 constant_dynamic-slice_fusion.2
  233.7 3.5 %convolution_multiply_fusion = f32[2,64,1024]{2,1,0:T(8,128)S(1)} fusion(bf16[2,1024,64]{1,2,0:T(8,128)(2,1)S(1)} %bitcast.84, bf16[2,1024,1024]{2,1,0:T(8,128)(2,1)} %bitcast.77), kind=kOutput, calls=%fused_computation.9 | convolution fusion | flops 268566528 | bytes 4980736 | tf_op jit(solution)/shard_map/mnr,mnc->mrc/dot_general | solution.py:73
  237.2 0.9 add.53
  238.1 1.4 convolution_multiply_fusion.1
  239.5 0.9 add.51
  240.3 27.4 %all-to-all-done.1 = bf16[32,2,16,1024]{3,2,1,0:T(8,128)(2,1)S(1)} async-done(((bf16[32,2,16,1024]{3,2,1,0:T(8,128)(2,1)}), bf16[32,2,16,1024]{3,2,1,0:T(8,128)(2,1)S(1)}, u32[]{:S(2)}, u32[]{:S(2)}) %all-to-all-start.1) | async-done | bytes 2097184 | tf_op jit(solution)/shard_map/all_to_all | solution.py:89
  267.7 1.2 fusion.5
  268.9 0.7 reshape.118
  (31 shorter events, 1.2 us)
Async XLA Ops:
  7.2 176.2 %copy-start = (bf16[2,4,1,16,1024]{4,3,2,1,0:T(8,128)(2,1)S(1)}, bf16[2,4,1,16,1024]{4,3,2,1,0:T(8,128)(2,1)}, u32[]{:S(2)}) copy-start(bf16[2,4,1,16,1024]{4,3,2,1,0:T(8,128)(2,1)} %param.10) | copy-start | bytes 786436
  7.2 71.7 %reduce-scatter.2.cloned.1.call-start = ((), (), s32[]{:S(2)}) async-start(), calls=%async_computation.3 | async-start | bytes 2228224 | tf_op jit(solution)/shard_map/reduce_scatter | solution.py:32
  7.9 132.7 %all-gather.4.cloned.1.call-start = ((), (), s32[]{:S(2)}) async-start(), calls=%async_computation.4 | async-start | bytes 4456448 | tf_op jit(solution)/shard_map/all_gather | solution.py:29
  80.7 12.4 %copy-start.7 = (s32[32]{0:T(128)S(1)}, s32[32]{0:T(128)}, u32[]{:S(2)}) copy-start(s32[32]{0:T(128)} %param.7) | copy-start | bytes 388
  80.7 59.7 %copy-start.6 = (s32[3]{0:T(128)S(1)}, s32[3]{0:T(128)}, u32[]{:S(2)}) copy-start(s32[3]{0:T(128)} %constant.55.clone.1) | copy-start | bytes 40
  83.2 55.9 %all-to-all-start = ((bf16[32,2,16,1024]{3,2,1,0:T(8,128)(2,1)}), bf16[32,2,16,1024]{3,2,1,0:T(8,128)(2,1)S(1)}, u32[]{:S(2)}, u32[]{:S(2)}) async-start(bf16[32,2,16,1024]{3,2,1,0:T(8,128)(2,1)} %bitcast.3), calls=%async_computation.1 | async-start | bytes 4194304 | tf_op jit(solution)/shard_map/all_to_all | solution.py:54
  93.1 90.3 %all-gather.6.cloned.1.call-start = ((), (), s32[]{:S(2)}) async-start(), calls=%async_computation.5 | async-start | bytes 4456448 | tf_op jit(solution)/shard_map/all_gather | solution.py:60
  183.4 6.7 %copy-start.5 = (s32[4]{0:T(128)S(1)}, s32[4]{0:T(128)}, u32[]{:S(2)}) copy-start(s32[4]{0:T(128)} %constant.139) | copy-start | bytes 52
  207.5 60.3 %all-to-all-start.1 = ((bf16[32,2,16,1024]{3,2,1,0:T(8,128)(2,1)}), bf16[32,2,16,1024]{3,2,1,0:T(8,128)(2,1)S(1)}, u32[]{:S(2)}, u32[]{:S(2)}) async-start(bf16[32,2,16,1024]{3,2,1,0:T(8,128)(2,1)} %bitcast.10), calls=%async_computation.2 | async-start | bytes 4194304 | tf_op jit(solution)/shard_map/all_to_all | solution.py:89
  232.6 4.6 %copy-start.3 = (f32[2,4,1,16,1024]{4,3,2,1,0:T(8,128)S(1)}, f32[2,4,1,16,1024]{4,3,2,1,0:T(8,128)}, u32[]{:S(2)}) copy-start(f32[2,4,1,16,1024]{4,3,2,1,0:T(8,128)} %param.9) | copy-start | bytes 1572868
  232.6 5.5 %copy-start.1 = (bf16[2,4,256,1024]{3,2,1,0:T(8,128)(2,1)S(1)}, bf16[2,4,256,1024]{3,2,1,0:T(8,128)(2,1)}, u32[]{:S(2)}) copy-start(bf16[2,4,256,1024]{3,2,1,0:T(8,128)(2,1)} %all-gather.6.cloned.1.call-done) | copy-start | bytes 12582916
  232.6 5.5 %copy-start.2 = (bf16[2,4,16,1024]{3,2,1,0:T(8,128)(2,1)S(1)}, bf16[2,4,16,1024]{3,2,1,0:T(8,128)(2,1)}, u32[]{:S(2)}) copy-start(bf16[2,4,16,1024]{3,2,1,0:T(8,128)(2,1)} %gather_fusion) | copy-start | bytes 786436
  237.2 2.3 copy-start.4
Sparse Core Ops, SparseCore 0:
  10.8 68.0 reduce-scatter.1
  81.0 42.9 all-gather.3
  140.6 42.7 all-gather.5
where the time goes:
time: 277 us; the launch traced here: 276 us
  waiting for transfers between devices  187 us (68%)
  local copies, waits for them, and re-layouts  30.1 us (11%)
  starting transfers between devices  19.8 us (7%)
  between operations  13.9 us (5%)
  other arithmetic  13.7 us (5%)
  matrix products  12 us (4%)
    reduce_scatter x1, waiting for transfers between devices, on_device(): lax.psum_scatter(replica_grads[0].astype(jnp.float32).astype(jnp.bfloat16...  69.5 us
    all_to_all x1, waiting for transfers between devices, on_device(): lax.all_to_all(outgoing, 'fsdp', split_axis=0, concat_axis=0, tiled=True)  45.8 us
    all_gather x1, waiting for transfers between devices, on_device(): lax.all_gather(owned_rows, 'dp', axis=2, tiled=True)  42.7 us
    all_to_all x1, waiting for transfers between devices, on_device(): lax.all_to_all(homeward, 'fsdp', split_axis=0, concat_axis=0, tiled=True)  27.4 us
    scatter x4, other arithmetic  11.7 us
    all_to_all x1, starting transfers between devices, on_device(): lax.all_to_all(outgoing, 'fsdp', split_axis=0, concat_axis=0, tiled=True)  9.83 us
    all_to_all x1, starting transfers between devices, on_device(): lax.all_to_all(homeward, 'fsdp', split_axis=0, concat_axis=0, tiled=True)  9.82 us
    another operation x1, local copies, waits for them, and re-layouts, on_device(): entire.reshape(slots_here, block_size, sub_blocks, groups, strip_rows)  7.75 us
  transfers between devices with their start and end apart: 5, of which 4 were waited for; matrix products, arithmetic and copies ran while one was open for 11% of the time, Pallas kernels for 0%

commit v1 on v0

--- a/solution.py
+++ b/solution.py
@@ -57,9 +57,8 @@
         in_axes=(1, 0),
     )(arrived, first_band)
     owned_rows = owned_rows.reshape(slots_here, sub_blocks, 1, strip_rows, block_size)
-    entire = lax.all_gather(owned_rows, "dp", axis=2, tiled=True).reshape(
-        slots_here, block_size, block_size
-    )
+    reach_the_packet = lambda vals: jnp.concatenate(lax.all_gather(vals, axis_name="dp"), axis=2)
+    entire = reach_the_packet(owned_rows).reshape(slots_here, block_size, block_size)
     my_rows = owned_rows.reshape(slots_here, sub_blocks * strip_rows, block_size)
     left_gram = jnp.einsum("mrc,mnc->mrn", my_rows, entire, preferred_element_type=jnp.float32)
     left_new = left_gram_state + (left_gram / block_size).reshape(left_gram_state.shape)

time: 277 us -> 329 us (1.19)
  the two profiles are of different devices: /device:TPU:16 before, /device:TPU:1 now
where the time goes in v1:
time: 329 us; the launch traced here: 327 us
  waiting for transfers between devices  202 us (61%)
  local copies, waits for them, and re-layouts  68.1 us (21%)
  starting transfers between devices  18.2 us (6%)
  between operations  13.9 us (4%)
  other arithmetic  13.6 us (4%)
  matrix products  11.7 us (4%)
    reduce_scatter x1, waiting for transfers between devices, on_device(): lax.psum_scatter(replica_grads[0].astype(jnp.float32).astype(jnp.bfloat16...  68.4 us
    all_gather x1, waiting for transfers between devices, on_device(): lax.all_gather(vals, axis_name='dp')  45.9 us
    all_to_all x1, waiting for transfers between devices, on_device(): lax.all_to_all(outgoing, 'fsdp', split_axis=0, concat_axis=0, tiled=True)  45.8 us
    all_gather x1, waiting for transfers between devices, on_device(): lax.all_gather(right_inverse_root, 'dp', axis=2, tiled=True)  40.3 us
    another operation x1, local copies, waits for them, and re-layouts, on_device(): entire.reshape(slots_here, block_size, sub_blocks, groups, strip_rows)  31.7 us
    dynamic_slice x2, local copies, waits for them, and re-layouts, on_device(): lax.dynamic_index_in_dim(entire.reshape(slots_here, block_size, sub_block...  17.7 us
    scatter x4, other arithmetic  11.6 us
    all_to_all x1, starting transfers between devices, on_device(): lax.all_to_all(outgoing, 'fsdp', split_axis=0, concat_axis=0, tiled=True)  9.06 us
  transfers between devices with their start and end apart: 5, of which 4 were waited for; matrix products, arithmetic and copies ran while one was open for 19% of the time, Pallas kernels for 0%

profile of v1, /device:TPU:1, one launch (start us, length us, event | category | flops | bytes accessed | tf_op | source)
XLA Modules:
  0.0 327.3 jit_solution(9164719099686930624)
XLA Ops:
  7.2 0.7 reduce-scatter.2.cloned.1.call-update
  7.9 0.7 dynamic_slice.7
  8.7 68.4 %reduce-scatter.2.cloned.1.call-done = bf16[16,4096]{1,0:T(8,128)(2,1)} async-done(((bf16[256,4096]{1,0:T(8,128)(2,1)}), bf16[16,4096]{1,0:T(8,128)(2,1)}) %reduce-scatter.2.cloned.1.call-update) | async-done | bytes 131088 | tf_op jit(solution)/shard_map/reduce_scatter | solution.py:32
  77.1 1.0 reshape.107
  78.1 0.8 convolution_convert_fusion
  78.9 2.5 copy.39
  81.4 9.1 %all-to-all-start = ((bf16[32,2,16,1024]{3,2,1,0:T(8,128)(2,1)}), bf16[32,2,16,1024]{3,2,1,0:T(8,128)(2,1)S(1)}, u32[]{:S(2)}, u32[]{:S(2)}) async-start(bf16[32,2,16,1024]{3,2,1,0:T(8,128)(2,1)} %bitcast.3), calls=%async_computation.1 | async-start | bytes 4194304 | tf_op jit(solution)/shard_map/all_to_all | solution.py:54
  90.8 45.8 %all-to-all-done = bf16[32,2,16,1024]{3,2,1,0:T(8,128)(2,1)S(1)} async-done(((bf16[32,2,16,1024]{3,2,1,0:T(8,128)(2,1)}), bf16[32,2,16,1024]{3,2,1,0:T(8,128)(2,1)S(1)}, u32[]{:S(2)}, u32[]{:S(2)}) %all-to-all-start) | async-done | bytes 2097184 | tf_op jit(solution)/shard_map/all_to_all | solution.py:54
  136.6 1.3 gather_fusion
  137.9 0.7 all-gather.4.cloned.1.call-update
  138.8 45.9 %all-gather.6.cloned.1.call-done = bf16[32,4,16,1024]{3,2,1,0:T(8,128)(2,1)} async-done(((bf16[2,4,16,1024]{3,2,1,0:T(8,128)(2,1)}), bf16[32,4,16,1024]{3,2,1,0:T(8,128)(2,1)}) %all-gather.6.cloned.1.call-update) | async-done | bytes 4194320 | tf_op jit(solution)/shard_map/all_gather | solution.py:60
  184.7 5.1 %copy.52 = bf16[16,2,4,1,16,1024]{5,4,0,2,1,3:T(8,128)(2,1)} copy(bf16[16,2,4,1,16,1024]{5,4,2,1,0,3:T(8,128)(2,1)} %bitcast.88) | data formatting | bytes 8388608 | tf_op jit(solution)/shard_map/all_gather | solution.py:60
  189.8 40.3 %all-gather.4.cloned.1.call-done = bf16[2,4,16,16,1024]{4,3,2,1,0:T(8,128)(2,1)} async-done(((bf16[2,4,1,16,1024]{4,3,2,1,0:T(8,128)(2,1)}), bf16[2,4,16,16,1024]{4,3,2,1,0:T(8,128)(2,1)}) %all-gather.4.cloned.1.call-update) | async-done | bytes 4194320 | tf_op jit(solution)/shard_map/all_gather | solution.py:29
  230.1 5.1 %convolution_convert_fusion.2 = bf16[2,64,1024]{2,1,0:T(8,128)(2,1)S(1)} fusion(bf16[2,1024,1024]{2,1,0:T(8,128)(2,1)} %bitcast.89, bf16[2,64,1024]{2,1,0:T(8,128)(2,1)S(1)} %bitcast.82, bf16[2,1024,1024]{2,1,0:T(8,128)(2,1)} %bitcast.83), kind=kOutput, calls=%fused_computation.12 | convolution fusion | flops 537133056 | bytes 8912896 | tf_op jit(solution)/shard_map/mrn,mnc->mrc/dot_general | solution.py:78
  235.2 1.6 broadcast_in_dim.16.clone
  236.8 17.2 %while.1 = (s32[]{:T(128)}, bf16[2,32,16,1024]{3,2,0,1:T(8,128)(2,1)}, s32[2,4]{1,0:T(2,128)S(1)}, bf16[2,4,16,1024]{3,2,1,0:T(8,128)(2,1)S(1)}, s32[]{:T(128)}, /*index=5*/s32[4]{0:T(128)S(1)}) while((s32[]{:T(128)}, bf16[2,32,16,1024]{3,2,0,1:T(8,128)(2,1)}, s32[2,4]{1,0:T(2,128)S(1)}, bf16[2,4,16,1024]{3,2,1,0:T(8,128)(2,1)S(1)}, s32[]{:T(128)}, ...), condition=%wide.while_cond, body=%wide.while_body.sunk | while | flops 65565 | bytes 657586 | solution.py:83
  237.5 3.3 and_reduce_fusion.2
  240.8 2.1 constant_dynamic-slice_fusion.6
  242.9 2.5 bitcast_dynamic-update-slice_fusion.2
  246.1 3.3 and_reduce_fusion.2
  249.3 2.1 constant_dynamic-slice_fusion.6
  251.5 2.5 bitcast_dynamic-update-slice_fusion.2
  254.0 9.0 %all-to-all-start.1 = ((bf16[32,2,16,1024]{3,2,1,0:T(8,128)(2,1)}), bf16[32,2,16,1024]{3,2,1,0:T(8,128)(2,1)S(1)}, u32[]{:S(2)}, u32[]{:S(2)}) async-start(bf16[32,2,16,1024]{3,2,1,0:T(8,128)(2,1)} %bitcast.12), calls=%async_computation.2 | async-start | bytes 4194304 | tf_op jit(solution)/shard_map/all_to_all | solution.py:88
  263.1 31.7 %reshape_reshape_reshape.3 = bf16[2,1024,4,16,16]{4,3,2,1,0:T(8,128)(2,1)} reshape(bf16[2,4,16,1,16,1024]{5,4,2,1,0,3:T(8,128)(2,1)} %bitcast.84) | data formatting | bytes 8388608 | tf_op jit(solution)/shard_map/reshape;reshape;reshape | solution.py:66
  294.8 9.0 %constant_dynamic-slice_fusion.2 = bf16[2,1024,4,1,16]{4,3,2,1,0:T(2,128)(2,1)} fusion(bf16[2,1024,4,16,16]{4,3,2,1,0:T(8,128)(2,1)} %reshape_reshape_reshape.3, s32[]{:T(128)S(6)} %select_n.44), kind=kLoop, calls=%fused_computation.31 | loop fusion | bytes 524292 | tf_op jit(solution)/shard_map/jit(dynamic_index_in_dim)/dynamic_slice | solution.py:65
  303.8 8.7 %copy.37 = bf16[2,1024,4,1,16]{1,4,2,0,3:T(8,128)(2,1)S(1)} copy(bf16[2,1024,4,1,16]{4,3,2,1,0:T(2,128)(2,1)} %constant_dynamic-slice_fusion.2) | data formatting | bytes 524288 | tf_op jit(solution)/shard_map/jit(dynamic_index_in_dim)/dynamic_slice | solution.py:65
  312.5 3.2 convolution_multiply_fusion
  315.7 0.9 add.53
  316.6 1.4 convolution_multiply_fusion.1
  318.0 0.9 add.51
  318.8 1.2 fusion.5
  320.1 0.7 reshape.114
  (34 shorter events, 1.9 us)
Async XLA Ops:
  7.2 223.0 %copy-start = (bf16[2,4,1,16,1024]{4,3,2,1,0:T(8,128)(2,1)S(1)}, bf16[2,4,1,16,1024]{4,3,2,1,0:T(8,128)(2,1)}, u32[]{:S(2)}) copy-start(bf16[2,4,1,16,1024]{4,3,2,1,0:T(8,128)(2,1)} %param.10) | copy-start | bytes 786436
  7.2 69.9 %reduce-scatter.2.cloned.1.call-start = ((), (), s32[]{:S(2)}) async-start(), calls=%async_computation.3 | async-start | bytes 2228224 | tf_op jit(solution)/shard_map/reduce_scatter | solution.py:32
  78.9 11.6 %copy-start.8 = (s32[32]{0:T(128)S(1)}, s32[32]{0:T(128)}, u32[]{:S(2)}) copy-start(s32[32]{0:T(128)} %param.7) | copy-start | bytes 388
  78.9 59.7 %copy-start.7 = (s32[3]{0:T(128)S(1)}, s32[3]{0:T(128)}, u32[]{:S(2)}) copy-start(s32[3]{0:T(128)} %constant.55.clone.1) | copy-start | bytes 40
  81.4 55.2 %all-to-all-start = ((bf16[32,2,16,1024]{3,2,1,0:T(8,128)(2,1)}), bf16[32,2,16,1024]{3,2,1,0:T(8,128)(2,1)S(1)}, u32[]{:S(2)}, u32[]{:S(2)}) async-start(bf16[32,2,16,1024]{3,2,1,0:T(8,128)(2,1)} %bitcast.3), calls=%async_computation.1 | async-start | bytes 4194304 | tf_op jit(solution)/shard_map/all_to_all | solution.py:54
  90.5 94.3 %all-gather.6.cloned.1.call-start = ((), (), s32[]{:S(2)}) async-start(), calls=%async_computation.5 | async-start | bytes 4456448 | tf_op jit(solution)/shard_map/all_gather | solution.py:60
  137.9 92.2 %all-gather.4.cloned.1.call-start = ((), (), s32[]{:S(2)}) async-start(), calls=%async_computation.4 | async-start | bytes 4456448 | tf_op jit(solution)/shard_map/all_gather | solution.py:29
  230.1 6.7 %copy-start.6 = (s32[4]{0:T(128)S(1)}, s32[4]{0:T(128)}, u32[]{:S(2)}) copy-start(s32[4]{0:T(128)} %constant.139) | copy-start | bytes 52
  254.0 64.8 %all-to-all-start.1 = ((bf16[32,2,16,1024]{3,2,1,0:T(8,128)(2,1)}), bf16[32,2,16,1024]{3,2,1,0:T(8,128)(2,1)S(1)}, u32[]{:S(2)}, u32[]{:S(2)}) async-start(bf16[32,2,16,1024]{3,2,1,0:T(8,128)(2,1)} %bitcast.12), calls=%async_computation.2 | async-start | bytes 4194304 | tf_op jit(solution)/shard_map/all_to_all | solution.py:88
  303.8 11.9 %copy-start.4 = (f32[2,4,1,16,1024]{4,3,2,1,0:T(8,128)S(1)}, f32[2,4,1,16,1024]{4,3,2,1,0:T(8,128)}, u32[]{:S(2)}) copy-start(f32[2,4,1,16,1024]{4,3,2,1,0:T(8,128)} %param.9) | copy-start | bytes 1572868
  312.5 4.1 %copy-start.2 = (bf16[16,2,4,1,16,1024]{5,4,0,2,1,3:T(8,128)(2,1)S(1)}, bf16[16,2,4,1,16,1024]{5,4,0,2,1,3:T(8,128)(2,1)}, u32[]{:S(2)}) copy-start(bf16[16,2,4,1,16,1024]{5,4,0,2,1,3:T(8,128)(2,1)} %copy.52) | copy-start | bytes 12582916
  312.5 4.1 %copy-start.3 = (bf16[2,4,16,1024]{3,2,1,0:T(8,128)(2,1)S(1)}, bf16[2,4,16,1024]{3,2,1,0:T(8,128)(2,1)}, u32[]{:S(2)}) copy-start(bf16[2,4,16,1024]{3,2,1,0:T(8,128)(2,1)} %gather_fusion) | copy-start | bytes 786436
  315.7 2.3 copy-start.5
  316.6 4.2 %copy-start.1 = (bf16[2,4,1,16,1024]{4,3,2,1,0:T(8,128)(2,1)S(1)}, bf16[2,4,1,16,1024]{4,3,2,1,0:T(8,128)(2,1)}, u32[]{:S(2)}) copy-start(bf16[2,4,1,16,1024]{4,3,2,1,0:T(8,128)(2,1)} %param.10) | copy-start | bytes 786436
Sparse Core Ops, SparseCore 0:
  10.8 66.2 reduce-scatter.1
  138.0 46.6 all-gather.5
  186.9 43.2 all-gather.3
